TPU v7x, 32 devices: a whole 2x2x4 slice. The times are simulated.
32 devices in a mesh: row: 2 (over x), col: 16 (over z, y, core).
Axes of the slice: x: 2, y: 2, z: 4, core: 2. Of those that a mesh axis runs over, the one named last changes fastest.
Arguments:
- ld_matrix: bfloat16 [32768, 32768], P('row', 'col'), may hold values from -0.23925781 to 0.23925781
- factor: float32 [32768, 256], P(('row', 'col')), may hold values from -0.24 to 0.24
- diag_values: bfloat16 [32768], P('col'), may hold values from 0.5 to 4
Outputs:
- factor_grad: float32 [32768, 256], P(('row', 'col'))
All inputs are finite; a program needn't handle non-finite values.
Results may differ from a plain program's by a relative error of at most 0.003.
Values may be sent and summed in bfloat16 or wider, within the bound.
A program may use at most 128 MiB of HBM per device.

v0:
```python
import jax
import jax.numpy as jnp
from jax import lax
from jax.sharding import PartitionSpec as P


def local(ld_matrix, factor, diag_values):
    n_row, n_col = (lax.axis_size("row"), lax.axis_size("col"))
    row_index, col_index = (lax.axis_index("row"), lax.axis_index("col"))
    factor_low = factor.astype(jnp.bfloat16)
    own, rank = factor.shape
    width = ld_matrix.shape[1]
    panel = jnp.zeros((width, rank), jnp.bfloat16)
    for k in range(n_row):
        pairs = [
            (n_row * c + (r + k) % n_row, r * n_col + c) for r in range(n_row) for c in range(n_col)
        ]
        piece = lax.ppermute(factor_low, ("row", "col"), pairs)
        at = lax.rem(row_index + k, n_row) * own
        panel = lax.dynamic_update_slice_in_dim(panel, piece, at, 0)
    gram = lax.dot_general(
        factor_low, factor_low, (((0,), (0,)), ((), ())), preferred_element_type=jnp.float32
    )
    gram = lax.psum(gram, ("row", "col"))
    part = jnp.dot(ld_matrix, panel, preferred_element_type=jnp.float32)
    per_row = n_col // n_row
    first = col_index % per_row * width
    scale = jnp.where(row_index == col_index // per_row, diag_values, 0).astype(jnp.float32)
    slab = lax.dynamic_slice_in_dim(part, first, width, 0)
    slab = slab - scale[:, None] * panel.astype(jnp.float32)
    part = lax.dynamic_update_slice_in_dim(part, slab, first, 0).astype(jnp.bfloat16)
    total = lax.psum_scatter(part, "col", scatter_dimension=0, tiled=True)
    model = jnp.dot(
        factor_low, gram, precision=lax.Precision.HIGHEST, preferred_element_type=jnp.float32
    )
    return 4.0 * (model - total.astype(jnp.float32))


def solution(mesh):
    in_specs = (P("row", "col"), P(("row", "col"), None), P("col"))
    out_specs = P(("row", "col"), None)
    return jax.shard_map(local, mesh=mesh, in_specs=in_specs, out_specs=out_specs, check_vma=False)
```

profile of v0, /device:TPU:0, one launch (start us, length us, event | category | flops | bytes accessed | tf_op | source)
XLA Modules:
  0.0 220.3 jit_solution(2321519786538181490)
XLA Ops:
  7.4 0.0 all-reduce.2.cloned.1.call-start
  7.4 1.4 copy.4
  8.8 0.7 collective-permute-start
  9.5 6.8 %collective-permute-start.1 = (bf16[1024,256]{0,1:T(8,128)(2,1)S(1)}, bf16[1024,256]{0,1:T(8,128)(2,1)S(1)}, u32[]{:S(2)}, u32[]{:S(2)}) collective-permute-start(bf16[1024,256]{0,1:T(8,128)(2,1)S(1)} %copy.4), channel_id=1, source_target_pairs={{1,0},{3,1},{5,2},{7,3},{9,4},{11,5},{13,6},{15,7},{17,8},{19,9},{... | collective-permute-start | bytes 1572872 | tf_op jit(solution)/shard_map/ppermute | solution.py:18
  16.3 1.0 fusion.1
  17.3 0.0 all-reduce.2.cloned.1.call-update
  17.4 0.0 reduce-scatter.2.cloned.1.call-start
  17.5 0.7 select_convert_fusion
  18.2 0.0 collective-permute-done
  18.2 0.1 broadcast_in_dim.8
  18.3 0.1 constant_dynamic-update-slice_fusion.1
  18.3 17.3 %collective-permute-done.1 = bf16[1024,256]{0,1:T(8,128)(2,1)S(1)} collective-permute-done((bf16[1024,256]{0,1:T(8,128)(2,1)S(1)}, bf16[1024,256]{0,1:T(8,128)(2,1)S(1)}, u32[]{:S(2)}, u32[]{:S(2)}) %collective-permute-start.1) | collective-permute-done | bytes 524320 | tf_op jit(solution)/shard_map/ppermute | solution.py:18
  35.7 32.1 %fusion.2 = f32[256,16384]{1,0:T(8,128)} fusion(bf16[2048,256]{0,1:T(8,128)(2,1)S(1)} %constant_dynamic-update-slice_fusion, bf16[16384,2048]{1,0:T(8,128)(2,1)} %param.3), kind=kOutput, calls=%fused_computation.8 | convolution fusion | flops 17179869184 | bytes 84934656 | tf_op jit(solution)/shard_map/dot_general | solution.py:25
  67.8 5.8 %copy.9 = f32[16384,256]{0,1:T(8,128)S(1)} copy(f32[16384,256]{0,1:T(8,128)} %bitcast.13) | data formatting | bytes 33554432
  73.7 2.0 fusion
  75.7 3.7 %convert_element_type.20 = bf16[16384,256]{0,1:T(8,128)(2,1)} convert(f32[16384,256]{0,1:T(8,128)S(1)} %fusion) | non-fusion elementwise | flops 4194304 | bytes 25165824 | tf_op jit(solution)/shard_map/convert_element_type | solution.py:31
  79.4 0.0 reduce-scatter.2.cloned.1.call-update
  79.5 99.7 %all-reduce.2.cloned.1.call-done = f32[256,256]{1,0:T(8,128)} async-done(((f32[256,256]{1,0:T(8,128)}), f32[256,256]{1,0:T(8,128)}) %all-reduce.2.cloned.1.call-update) | async-done | bytes 262160 | tf_op jit(solution)/shard_map/psum | solution.py:24
  179.1 1.6 convolution_bitcast_fusion
  180.7 29.7 %reduce-scatter.2.cloned.1.call-done = bf16[1024,256]{0,1:T(8,128)(2,1)} async-done(((bf16[16384,256]{0,1:T(8,128)(2,1)}), bf16[1024,256]{0,1:T(8,128)(2,1)}) %reduce-scatter.2.cloned.1.call-update) | async-done | bytes 524304 | tf_op jit(solution)/shard_map/reduce_scatter | solution.py:32
  210.4 1.2 subtract_multiply_fusion
  211.6 1.3 copy.5
  (1 shorter events, 0.0 us)
Async XLA Ops:
  7.4 171.8 %all-reduce.2.cloned.1.call-start = ((), (), s32[]{:S(2)}) async-start(), calls=%async_computation.1 | async-start | bytes 524288 | tf_op jit(solution)/shard_map/psum | solution.py:24
  8.8 9.4 %collective-permute-start = (bf16[1024,256]{0,1:T(8,128)(2,1)S(1)}, bf16[1024,256]{0,1:T(8,128)(2,1)S(1)}, u32[]{:S(2)}, u32[]{:S(2)}) collective-permute-start(bf16[1024,256]{0,1:T(8,128)(2,1)S(1)} %copy.4), channel_id=1, source_target_pairs={{0,0},{2,1},{4,2},{6,3},{8,4},{10,5},{12,6},{14,7},{16,8},{18,9},{... | collective-permute-start | bytes 1572872 | tf_op jit(solution)/shard_map/ppermute | solution.py:18
  9.5 26.1 %collective-permute-start.1 = (bf16[1024,256]{0,1:T(8,128)(2,1)S(1)}, bf16[1024,256]{0,1:T(8,128)(2,1)S(1)}, u32[]{:S(2)}, u32[]{:S(2)}) collective-permute-start(bf16[1024,256]{0,1:T(8,128)(2,1)S(1)} %copy.4), channel_id=1, source_target_pairs={{1,0},{3,1},{5,2},{7,3},{9,4},{11,5},{13,6},{15,7},{17,8},{19,9},{... | collective-permute-start | bytes 1572872 | tf_op jit(solution)/shard_map/ppermute | solution.py:18
  17.4 193.0 %reduce-scatter.2.cloned.1.call-start = ((), (), s32[]{:S(2)}) async-start(), calls=%async_computation.2 | async-start | bytes 8912896 | tf_op jit(solution)/shard_map/reduce_scatter | solution.py:32
Sparse Core Ops, SparseCore 0:
  17.5 161.5 all-reduce.1
Sparse Core Ops, SparseCore 1:
  79.5 130.8 reduce-scatter.1
where the time goes:
time: 221 us; the launch traced here: 220 us
  waiting for transfers between devices  147 us (67%)
  matrix products  34.7 us (16%)
  between operations  14.9 us (7%)
  local copies, waits for them, and re-layouts  8.77 us (4%)
  other arithmetic  7.63 us (3%)
  starting transfers between devices  7.54 us (3%)
    psum x1, waiting for transfers between devices, local(): gram = lax.psum(gram, ('row', 'col'))  99.7 us
    dot_general x1, matrix products, local(): part = jnp.dot(ld_matrix, panel, preferred_element_type=jnp.float32)  32.1 us
    reduce_scatter x1, waiting for transfers between devices, local(): total = lax.psum_scatter(part, 'col', scatter_dimension=0, tiled=True)  29.7 us
    ppermute x2, waiting for transfers between devices, local(): piece = lax.ppermute(factor_low, ('row', 'col'), pairs)  17.3 us
    ppermute x2, starting transfers between devices, local(): piece = lax.ppermute(factor_low, ('row', 'col'), pairs)  7.49 us
    unnamed x2, local copies, waits for them, and re-layouts  7.26 us
  transfers between devices with their start and end apart: 4, of which 3 were waited for; matrix products, arithmetic and copies ran while one was open for 21% of the time, Pallas kernels for 0%

commit v1 on v0

--- a/solution.py
+++ b/solution.py
@@ -21,7 +21,7 @@
     gram = lax.dot_general(
         factor_low, factor_low, (((0,), (0,)), ((), ())), preferred_element_type=jnp.float32
     )
-    gram = lax.psum(gram, ("row", "col"))
+    gram = jnp.sum(lax.all_gather(gram, ("row", "col")), axis=0)
     part = jnp.dot(ld_matrix, panel, preferred_element_type=jnp.float32)
     per_row = n_col // n_row
     first = col_index % per_row * width

time: 221 us -> 239 us (1.081)
  waiting for transfers between devices: 147 us -> 161 us
  other arithmetic: 7.63 us -> 11.6 us
    psum x1 -> x0, waiting for transfers between devices: 99.7 us -> none  [local(): gram = lax.psum(gram, ('row', 'col'))]
    reduce_scatter x1, waiting for transfers between devices: 29.7 us -> 114 us  [local(): total = lax.psum_scatter(part, 'col', scatter_dimension=0, tiled=True)]
    all_gather x0 -> x1, waiting for transfers between devices: none -> 28.9 us  [local(): gram = jnp.sum(lax.all_gather(gram, ('row', 'col')), axis=0)]
    reduce_sum x0 -> x1, other arithmetic: none -> 3.93 us  [local(): gram = jnp.sum(lax.all_gather(gram, ('row', 'col')), axis=0)]
where the time goes in v1:
time: 239 us; the launch traced here: 238 us
  waiting for transfers between devices  161 us (67%)
  matrix products  33.8 us (14%)
  between operations  14.9 us (6%)
  other arithmetic  11.6 us (5%)
  local copies, waits for them, and re-layouts  8.73 us (4%)
  starting transfers between devices  7.54 us (3%)
    reduce_scatter x1, waiting for transfers between devices, local(): total = lax.psum_scatter(part, 'col', scatter_dimension=0, tiled=True)  114 us
    dot_general x1, matrix products, local(): part = jnp.dot(ld_matrix, panel, preferred_element_type=jnp.float32)  32.1 us
    all_gather x1, waiting for transfers between devices, local(): gram = jnp.sum(lax.all_gather(gram, ('row', 'col')), axis=0)  28.9 us
    ppermute x2, waiting for transfers between devices, local(): piece = lax.ppermute(factor_low, ('row', 'col'), pairs)  18.4 us
    ppermute x2, starting transfers between devices, local(): piece = lax.ppermute(factor_low, ('row', 'col'), pairs)  7.49 us
    unnamed x2, local copies, waits for them, and re-layouts  7.21 us
  transfers between devices with their start and end apart: 4, of which 3 were waited for; matrix products, arithmetic and copies ran while one was open for 21% of the time, Pallas kernels for 0%

profile of v1, /device:TPU:0, one launch (start us, length us, event | category | flops | bytes accessed | tf_op | source)
XLA Modules:
  0.0 238.1 jit_solution(14066603708535846430)
XLA Ops:
  7.4 0.0 all-gather.3.cloned.1.call-start
  7.4 1.4 copy.4
  8.8 1.0 fusion.1
  9.8 0.0 all-gather.3.cloned.1.call-update
  9.9 0.0 reduce-scatter.2.cloned.1.call-start
  9.9 0.7 collective-permute-start
  10.6 6.8 %collective-permute-start.1 = (bf16[1024,256]{0,1:T(8,128)(2,1)S(1)}, bf16[1024,256]{0,1:T(8,128)(2,1)S(1)}, u32[]{:S(2)}, u32[]{:S(2)}) collective-permute-start(bf16[1024,256]{0,1:T(8,128)(2,1)S(1)} %copy.4), channel_id=1, source_target_pairs={{1,0},{3,1},{5,2},{7,3},{9,4},{11,5},{13,6},{15,7},{17,8},{19,9},{... | collective-permute-start | bytes 1572872 | tf_op jit(solution)/shard_map/ppermute | solution.py:18
  17.4 0.7 select_convert_fusion
  18.1 0.0 collective-permute-done
  18.1 0.1 broadcast_in_dim.8
  18.2 0.1 constant_dynamic-update-slice_fusion.1
  18.3 18.4 %collective-permute-done.1 = bf16[1024,256]{0,1:T(8,128)(2,1)S(1)} collective-permute-done((bf16[1024,256]{0,1:T(8,128)(2,1)S(1)}, bf16[1024,256]{0,1:T(8,128)(2,1)S(1)}, u32[]{:S(2)}, u32[]{:S(2)}) %collective-permute-start.1) | collective-permute-done | bytes 524320 | tf_op jit(solution)/shard_map/ppermute | solution.py:18
  36.7 32.1 %fusion.2 = f32[256,16384]{1,0:T(8,128)} fusion(bf16[2048,256]{0,1:T(8,128)(2,1)S(1)} %constant_dynamic-update-slice_fusion, bf16[16384,2048]{1,0:T(8,128)(2,1)} %param.3), kind=kOutput, calls=%fused_computation.8 | convolution fusion | flops 17179869184 | bytes 84934656 | tf_op jit(solution)/shard_map/dot_general | solution.py:25
  68.9 5.8 %copy.8 = f32[16384,256]{0,1:T(8,128)S(1)} copy(f32[16384,256]{0,1:T(8,128)} %bitcast.14) | data formatting | bytes 33554432
  74.7 2.0 fusion
  76.7 3.8 %convert_element_type.20 = bf16[16384,256]{0,1:T(8,128)(2,1)} convert(f32[16384,256]{0,1:T(8,128)S(1)} %fusion) | non-fusion elementwise | flops 4194304 | bytes 25165824 | tf_op jit(solution)/shard_map/convert_element_type | solution.py:31
  80.5 0.0 reduce-scatter.2.cloned.1.call-update
  80.5 28.9 %all-gather.3.cloned.1.call-done = f32[8192,256]{1,0:T(8,128)} async-done(((f32[256,256]{1,0:T(8,128)}), f32[8192,256]{1,0:T(8,128)}) %all-gather.3.cloned.1.call-update) | async-done | bytes 8388624 | tf_op jit(solution)/shard_map/all_gather | solution.py:24
  109.4 3.9 %reduce_sum.9 = f32[256,256]{1,0:T(8,128)S(1)} reduce(f32[32,256,256]{2,1,0:T(8,128)} %bitcast.15, f32[]{:T(128)} %constant.40.clone.1), dimensions={0}, to_apply=%region_0.0 | reduce | flops 2031616 | bytes 8650756 | tf_op jit(solution)/shard_map/reduce_sum | solution.py:24
  113.3 0.6 convolution_bitcast_fusion
  113.9 114.2 %reduce-scatter.2.cloned.1.call-done = bf16[1024,256]{0,1:T(8,128)(2,1)} async-done(((bf16[16384,256]{0,1:T(8,128)(2,1)}), bf16[1024,256]{0,1:T(8,128)(2,1)}) %reduce-scatter.2.cloned.1.call-update) | async-done | bytes 524304 | tf_op jit(solution)/shard_map/reduce_scatter | solution.py:32
  228.1 1.2 subtract_multiply_fusion
  229.3 1.3 copy.5
  (1 shorter events, 0.0 us)
Async XLA Ops:
  7.4 102.0 %all-gather.3.cloned.1.call-start = ((), (), s32[]{:S(2)}) async-start(), calls=%async_computation.2 | async-start | bytes 8650752 | tf_op jit(solution)/shard_map/all_gather | solution.py:24
  9.9 218.2 %reduce-scatter.2.cloned.1.call-start = ((), (), s32[]{:S(2)}) async-start(), calls=%async_computation.1 | async-start | bytes 8912896 | tf_op jit(solution)/shard_map/reduce_scatter | solution.py:32
  9.9 8.2 %collective-permute-start = (bf16[1024,256]{0,1:T(8,128)(2,1)S(1)}, bf16[1024,256]{0,1:T(8,128)(2,1)S(1)}, u32[]{:S(2)}, u32[]{:S(2)}) collective-permute-start(bf16[1024,256]{0,1:T(8,128)(2,1)S(1)} %copy.4), channel_id=1, source_target_pairs={{0,0},{2,1},{4,2},{6,3},{8,4},{10,5},{12,6},{14,7},{16,8},{18,9},{... | collective-permute-start | bytes 1572872 | tf_op jit(solution)/shard_map/ppermute | solution.py:18
  10.6 26.1 %collective-permute-start.1 = (bf16[1024,256]{0,1:T(8,128)(2,1)S(1)}, bf16[1024,256]{0,1:T(8,128)(2,1)S(1)}, u32[]{:S(2)}, u32[]{:S(2)}) collective-permute-start(bf16[1024,256]{0,1:T(8,128)(2,1)S(1)} %copy.4), channel_id=1, source_target_pairs={{1,0},{3,1},{5,2},{7,3},{9,4},{11,5},{13,6},{15,7},{17,8},{19,9},{... | collective-permute-start | bytes 1572872 | tf_op jit(solution)/shard_map/ppermute | solution.py:18
Sparse Core Ops, SparseCore 0:
  11.0 98.2 all-gather.2
Sparse Core Ops, SparseCore 1:
  80.6 147.5 reduce-scatter.1

commit v2 on v0

--- a/solution.py
+++ b/solution.py
@@ -21,7 +21,7 @@
     gram = lax.dot_general(
         factor_low, factor_low, (((0,), (0,)), ((), ())), preferred_element_type=jnp.float32
     )
-    gram = lax.psum(gram, ("row", "col"))
+    gram = lax.psum(lax.psum(gram, "col"), "row")
     part = jnp.dot(ld_matrix, panel, preferred_element_type=jnp.float32)
     per_row = n_col // n_row
     first = col_index % per_row * width

time: 221 us -> 275 us (1.24)
  waiting for transfers between devices: 147 us -> 203 us
    reduce_scatter x1, waiting for transfers between devices: 29.7 us -> 103 us  [local(): total = lax.psum_scatter(part, 'col', scatter_dimension=0, tiled=True)]
    ppermute x2, waiting for transfers between devices: 17.3 us -> 0.01 us  [local(): piece = lax.ppermute(factor_low, ('row', 'col'), pairs)]
    psum x1 -> x2, waiting for transfers between devices: 99.7 us -> 99.8 us  [local(): gram = lax.psum(lax.psum(gram, 'col'), 'row')]
  transfers between devices with their start and end apart: 4 -> 5, of which waited for: 3 -> 2; matrix products, arithmetic and copies ran while one was open for 21% -> 17% of each run, Pallas kernels for 0% -> 0%
where the time goes in v2:
time: 275 us; the launch traced here: 274 us
  waiting for transfers between devices  203 us (74%)
  matrix products  34.7 us (13%)
  between operations  13.2 us (5%)
  local copies, waits for them, and re-layouts  8.71 us (3%)
  other arithmetic  7.63 us (3%)
  starting transfers between devices  7.58 us (3%)
    reduce_scatter x1, waiting for transfers between devices, local(): total = lax.psum_scatter(part, 'col', scatter_dimension=0, tiled=True)  103 us
    psum x2, waiting for transfers between devices, local(): gram = lax.psum(lax.psum(gram, 'col'), 'row')  99.8 us
    dot_general x1, matrix products, local(): part = jnp.dot(ld_matrix, panel, preferred_element_type=jnp.float32)  32.1 us
    ppermute x2, starting transfers between devices, local(): piece = lax.ppermute(factor_low, ('row', 'col'), pairs)  7.49 us
    unnamed x2, local copies, waits for them, and re-layouts  7.2 us
  transfers between devices with their start and end apart: 5, of which 2 were waited for; matrix products, arithmetic and copies ran while one was open for 17% of the time, Pallas kernels for 0%

profile of v2, /device:TPU:0, one launch (start us, length us, event | category | flops | bytes accessed | tf_op | source)
XLA Modules:
  0.0 274.4 jit_solution(16317564804554738598)
XLA Ops:
  6.5 0.0 all-reduce.3.cloned.1.call-start
  6.5 1.4 copy.4
  8.0 0.7 collective-permute-start
  8.7 6.8 %collective-permute-start.1 = (bf16[1024,256]{0,1:T(8,128)(2,1)S(1)}, bf16[1024,256]{0,1:T(8,128)(2,1)S(1)}, u32[]{:S(2)}, u32[]{:S(2)}) collective-permute-start(bf16[1024,256]{0,1:T(8,128)(2,1)S(1)} %copy.4), channel_id=1, source_target_pairs={{1,0},{3,1},{5,2},{7,3},{9,4},{11,5},{13,6},{15,7},{17,8},{19,9},{... | collective-permute-start | bytes 1572872 | tf_op jit(solution)/shard_map/ppermute | solution.py:18
  15.5 1.0 fusion.1
  16.5 0.0 all-reduce.3.cloned.1.call-update
  16.5 0.0 all-reduce.5.cloned.1.call-start
  16.6 0.7 select_convert_fusion
  17.3 99.8 %all-reduce.3.cloned.1.call-done = f32[256,256]{1,0:T(8,128)} async-done(((f32[256,256]{1,0:T(8,128)}), f32[256,256]{1,0:T(8,128)}) %all-reduce.3.cloned.1.call-update) | async-done | bytes 262160 | tf_op jit(solution)/shard_map/psum | solution.py:24
  117.1 0.0 all-reduce.5.cloned.1.call-update
  117.1 0.0 reduce-scatter.2.cloned.1.call-start
  117.2 0.0 collective-permute-done
  117.2 0.1 broadcast_in_dim.8
  117.3 0.1 constant_dynamic-update-slice_fusion.1
  117.4 0.0 collective-permute-done.1
  117.4 0.1 constant_dynamic-update-slice_fusion
  117.5 32.1 %fusion.2 = f32[256,16384]{1,0:T(8,128)} fusion(bf16[2048,256]{0,1:T(8,128)(2,1)S(1)} %constant_dynamic-update-slice_fusion, bf16[16384,2048]{1,0:T(8,128)(2,1)} %param.3), kind=kOutput, calls=%fused_computation.8 | convolution fusion | flops 17179869184 | bytes 84934656 | tf_op jit(solution)/shard_map/dot_general | solution.py:25
  149.5 5.8 %copy.10 = f32[16384,256]{0,1:T(8,128)S(1)} copy(f32[16384,256]{0,1:T(8,128)} %bitcast.13) | data formatting | bytes 33554432
  155.3 2.0 fusion
  157.3 3.7 %convert_element_type.20 = bf16[16384,256]{0,1:T(8,128)(2,1)} convert(f32[16384,256]{0,1:T(8,128)S(1)} %fusion) | non-fusion elementwise | flops 4194304 | bytes 25165824 | tf_op jit(solution)/shard_map/convert_element_type | solution.py:31
  161.1 0.0 reduce-scatter.2.cloned.1.call-update
  161.1 0.0 all-reduce.5.cloned.1.call-done
  161.1 1.6 convolution_bitcast_fusion
  162.7 102.7 %reduce-scatter.2.cloned.1.call-done = bf16[1024,256]{0,1:T(8,128)(2,1)} async-done(((bf16[16384,256]{0,1:T(8,128)(2,1)}), bf16[1024,256]{0,1:T(8,128)(2,1)}) %reduce-scatter.2.cloned.1.call-update) | async-done | bytes 524304 | tf_op jit(solution)/shard_map/reduce_scatter | solution.py:32
  265.4 1.2 subtract_multiply_fusion
  266.6 1.3 copy.5
Async XLA Ops:
  6.5 110.6 %all-reduce.3.cloned.1.call-start = ((), (), s32[]{:S(2)}) async-start(), calls=%async_computation.1 | async-start | bytes 524288 | tf_op jit(solution)/shard_map/psum | solution.py:24
  8.0 109.2 %collective-permute-start = (bf16[1024,256]{0,1:T(8,128)(2,1)S(1)}, bf16[1024,256]{0,1:T(8,128)(2,1)S(1)}, u32[]{:S(2)}, u32[]{:S(2)}) collective-permute-start(bf16[1024,256]{0,1:T(8,128)(2,1)S(1)} %copy.4), channel_id=1, source_target_pairs={{0,0},{2,1},{4,2},{6,3},{8,4},{10,5},{12,6},{14,7},{16,8},{18,9},{... | collective-permute-start | bytes 1572872 | tf_op jit(solution)/shard_map/ppermute | solution.py:18
  8.7 108.7 %collective-permute-start.1 = (bf16[1024,256]{0,1:T(8,128)(2,1)S(1)}, bf16[1024,256]{0,1:T(8,128)(2,1)S(1)}, u32[]{:S(2)}, u32[]{:S(2)}) collective-permute-start(bf16[1024,256]{0,1:T(8,128)(2,1)S(1)} %copy.4), channel_id=1, source_target_pairs={{1,0},{3,1},{5,2},{7,3},{9,4},{11,5},{13,6},{15,7},{17,8},{19,9},{... | collective-permute-start | bytes 1572872 | tf_op jit(solution)/shard_map/ppermute | solution.py:18
  16.5 144.6 %all-reduce.5.cloned.1.call-start = ((), (), s32[]{:S(2)}) async-start(), calls=%async_computation.2 | async-start | bytes 524288 | tf_op jit(solution)/shard_map/psum | solution.py:24
  117.1 148.2 %reduce-scatter.2.cloned.1.call-start = ((), (), s32[]{:S(2)}) async-start(), calls=%async_computation.3 | async-start | bytes 8912896 | tf_op jit(solution)/shard_map/reduce_scatter | solution.py:32
Sparse Core Ops, SparseCore 0:
  16.7 100.4 all-reduce.2
  119.4 23.7 all-reduce.4
  161.2 104.1 reduce-scatter.1
